TPU v7x, 32 devices: a whole 2x2x4 slice. The times are simulated.
32 devices in a mesh: row: 8 (over z, core), col: 4 (over y, x).
Axes of the slice: x: 2, y: 2, z: 4, core: 2. Of those that a mesh axis runs over, the one named last changes fastest.
Arguments:
- x_fwd: bfloat16 [512, 6144], P('row', 'col'), may hold values from -6 to 6
- x_bwd: bfloat16 [512, 6144], P('row', 'col'), may hold values from -6 to 6
- grad_out: bfloat16 [512, 6144], P('row', 'col'), may hold values from -1.5 to 1.5
- gain: float32 [6144], P('col'), may hold values from 0.1 to 1.9
- w_up: bfloat16 [6144, 12288], P('col', 'row'), may hold values from -0.078125 to 0.078125
- w_down: bfloat16 [12288, 6144], P('row', 'col'), may hold values from -0.0546875 to 0.0546875
Outputs:
- y_fwd: bfloat16 [512, 6144], P('row', 'col')
- dx_bwd: bfloat16 [512, 6144], P('row', 'col')
- step_up: float32 [6144, 12288], P('col', 'row')
- step_down: float32 [12288, 6144], P('row', 'col')
- step_gain: float32 [6144], P('col')
- grad_rms: float32 [], replicated
All inputs are finite; a program needn't handle non-finite values.
Results may differ from a plain program's by a relative error of at most 0.0017.
The roundings to bfloat16 on the way count: a program that leaves them out, or rounds other values in their place, can miss the bound.
Values may be sent and summed in bfloat16 or wider, within the bound.
A program may use at most 128 MiB of HBM per device.

v0:
```python
import math
import jax
import jax.numpy as jnp
from jax import lax
from jax.sharding import PartitionSpec as P

D = 6144
FF = 12288
eps = 1e-06
clip_share = 0.25


def erf_gelu(value):
    return 0.5 * value * (1.0 + lax.erf(value * 0.7071067811865476))


def gelu_slope(value):
    return (
        0.5 * (1.0 + lax.erf(value * 0.7071067811865476))
        + value * jnp.exp(-0.5 * value * value) * 0.3989422804014327
    )


def contract(left, right, left_dim, right_dim):
    return lax.dot_general(
        left, right, (((left_dim,), (right_dim,)), ((), ())), preferred_element_type=jnp.float32
    )


def row_sums(tokens):
    values = tokens.astype(jnp.float32)
    return (jnp.sum(values, -1), jnp.sum(values * values, -1))


def normalize(tokens, first, second):
    values = tokens.astype(jnp.float32)
    centre = first / D
    spread = second / D - centre * centre
    inv_scale = lax.rsqrt(spread + eps)
    return ((values - centre[:, None]) * inv_scale[:, None], inv_scale)


def up_both(normed_a, normed_b, w_up):
    full_a, full_b = (
        lax.all_gather(normed_a, "row", axis=0, tiled=True),
        lax.all_gather(normed_b, "row", axis=0, tiled=True),
    )
    width = w_up.shape[1]
    summed = lax.psum_scatter(
        jnp.concatenate(
            [
                jnp.dot(full_a, w_up, preferred_element_type=jnp.float32),
                jnp.dot(full_b, w_up, preferred_element_type=jnp.float32),
            ],
            1,
        ),
        "col",
        scatter_dimension=0,
        tiled=True,
    )
    return (summed[:, :width], summed[:, width:], full_b)


def on_device(x_fwd, x_bwd, grad_out, gain, w_up, w_down):
    first_a, second_a = row_sums(x_fwd)
    first_b, second_b = row_sums(x_bwd)
    first_a, second_a, first_b, second_b = lax.psum((first_a, second_a, first_b, second_b), "col")
    centred_a, _ = normalize(x_fwd, first_a, second_a)
    centred_b, inv_scale = normalize(x_bwd, first_b, second_b)
    normed_a = (centred_a * gain).astype(jnp.bfloat16)
    normed_b = (centred_b * gain).astype(jnp.bfloat16)
    pre_a, pre_b, normed_full = up_both(normed_a, normed_b, w_up)
    hidden_a = erf_gelu(pre_a).astype(jnp.bfloat16)
    output_part = jnp.dot(
        lax.all_gather(hidden_a, "col", axis=0, tiled=True),
        w_down,
        preferred_element_type=jnp.float32,
    )
    output_sum = lax.psum_scatter(output_part, "row", scatter_dimension=0, tiled=True)
    y_fwd = (x_fwd.astype(jnp.float32) + output_sum).astype(jnp.bfloat16)
    hidden_b = erf_gelu(pre_b).astype(jnp.bfloat16)
    grad_full = lax.all_gather(grad_out, "row", axis=0, tiled=True)
    grad_hidden = lax.psum_scatter(
        contract(grad_full, w_down, 1, 1), "col", scatter_dimension=0, tiled=True
    )
    grad_pre = (grad_hidden * gelu_slope(pre_b)).astype(jnp.bfloat16)
    hidden_piece = lax.all_gather(hidden_b, "col", axis=0, tiled=True)
    pre_piece = lax.all_gather(grad_pre, "col", axis=0, tiled=True)
    down_total = contract(hidden_piece, grad_full, 0, 0)
    up_total = contract(normed_full, pre_piece, 0, 0)
    input_total = contract(pre_piece, w_up, 1, 1)
    grad_normed = lax.psum_scatter(input_total, "row", scatter_dimension=0, tiled=True)
    scaled = grad_normed * gain
    first_back = jnp.sum(scaled, -1)
    second_back = jnp.sum(scaled * centred_b, -1)
    first_back, second_back = lax.psum((first_back, second_back), "col")
    dx_bwd = (
        grad_out.astype(jnp.float32)
        + inv_scale[:, None]
        * (scaled - first_back[:, None] / D - centred_b * (second_back[:, None] / D))
    ).astype(jnp.bfloat16)
    gain_part = jnp.sum(grad_normed * centred_b, 0)
    weight_squares = jnp.sum(up_total * up_total) + jnp.sum(down_total * down_total)
    g_gain = lax.psum(gain_part, "row")
    first_row = (lax.axis_index("row") == 0).astype(jnp.float32)
    total = lax.psum(weight_squares + first_row * jnp.sum(g_gain * g_gain), ("row", "col"))
    param_count = 2 * D * FF + D
    norm_value = jnp.sqrt(total)
    grad_rms = norm_value / math.sqrt(param_count)
    factor = jnp.minimum(1.0, clip_share * math.sqrt(param_count) / norm_value)
    return (y_fwd, dx_bwd, up_total * factor, down_total * factor, g_gain * factor, grad_rms)


def solution(mesh):
    placed = (
        P("row", "col"),
        P("row", "col"),
        P("row", "col"),
        P("col"),
        P("col", "row"),
        P("row", "col"),
    )
    return jax.shard_map(
        on_device,
        mesh=mesh,
        in_specs=placed,
        out_specs=(
            P("row", "col"),
            P("row", "col"),
            P("col", "row"),
            P("row", "col"),
            P("col"),
            P(),
        ),
        check_vma=False,
    )
```

profile of v0, /device:TPU:0, one launch (start us, length us, event | category | flops | bytes accessed | tf_op | source)
XLA Modules:
  0.0 446.6 jit_solution(12459251885347289089)
XLA Ops:
  7.2 0.0 all-gather.13.cloned.1.call-start
  7.2 0.7 all-gather.13.cloned.1.call-update
  7.9 0.0 all-gather.7.cloned.1.call-start
  7.9 1.1 convert_reduce_fusion
  9.0 1.1 convert_reduce_fusion.1
  10.1 11.4 %all-reduce.1 = (f32[64]{0:T(128)S(1)}, f32[64]{0:T(128)S(1)}, f32[64]{0:T(128)S(1)}, f32[64]{0:T(128)S(1)}) all-reduce(f32[64]{0:T(128)S(1)} %get-tuple-element.12, f32[64]{0:T(128)S(1)} %get-tuple-element.11, f32[64]{0:T(128)S(1)} %get-tuple-element.10, f32[64]{0:T(128)S(1)} %get-tuple-element.9), channel_id=1, replica_groups=mesh['row'=8,'col'=4] {'col'}, use_global_device_ids=true, to_apply=%region_7.0 | all-reduce | flops 256 | bytes 2048 | tf_op jit(solution)/shard_map/psum | solution.py:67
  21.5 2.0 fusion.21
  23.6 0.0 all-gather.9.cloned.1.call-start
  23.6 0.7 all-gather.9.cloned.1.call-update
  24.3 0.0 reduce-scatter.9.cloned.1.call-start
  24.4 13.3 %all-gather.13.cloned.1.call-done = bf16[512,1536]{1,0:T(8,128)(2,1)} async-done(((bf16[64,1536]{1,0:T(8,128)(2,1)}), bf16[512,1536]{1,0:T(8,128)(2,1)}) %all-gather.13.cloned.1.call-update) | async-done | bytes 1572880 | tf_op jit(solution)/shard_map/all_gather | solution.py:82
  37.6 7.1 %fusion.27 = f32[512,1536]{1,0:T(8,128)} fusion(bf16[512,1536]{1,0:T(8,128)(2,1)} %all-gather.13.cloned.1.call-done, bf16[1536,1536]{1,0:T(8,128)(2,1)} %param.11), kind=kOutput, calls=%fused_computation.52 | convolution fusion | flops 2415919104 | bytes 9437184 | tf_op jit(solution)/shard_map/dot_general | solution.py:25
  44.8 0.0 reduce-scatter.5.cloned.1.call-start
  44.8 19.4 %all-gather.7.cloned.1.call-done = bf16[512,1536]{1,0:T(8,128)(2,1)} async-done(((bf16[64,1536]{1,0:T(8,128)(2,1)}), bf16[512,1536]{1,0:T(8,128)(2,1)}) %all-gather.7.cloned.1.call-update) | async-done | bytes 1572880 | tf_op jit(solution)/shard_map/all_gather | solution.py:45
  64.3 4.9 %fusion.24 = f32[512,1536]{1,0:T(8,128)S(1)} fusion(bf16[512,1536]{1,0:T(8,128)(2,1)} %all-gather.7.cloned.1.call-done, bf16[1536,1536]{1,0:T(8,128)(2,1)} %param.10), kind=kOutput, calls=%fused_computation.49 | convolution fusion | flops 2415919104 | bytes 9437184 | tf_op jit(solution)/shard_map/dot_general | solution.py:52
  69.2 21.7 %all-gather.9.cloned.1.call-done = bf16[512,1536]{1,0:T(8,128)(2,1)} async-done(((bf16[64,1536]{1,0:T(8,128)(2,1)}), bf16[512,1536]{1,0:T(8,128)(2,1)}) %all-gather.9.cloned.1.call-update) | async-done | bytes 1572880 | tf_op jit(solution)/shard_map/all_gather | solution.py:46
  90.9 4.9 %fusion.25 = f32[512,1536]{1,0:T(8,128)S(1)} fusion(bf16[512,1536]{1,0:T(8,128)(2,1)} %all-gather.9.cloned.1.call-done, bf16[1536,1536]{1,0:T(8,128)(2,1)} %param.10), kind=kOutput, calls=%fused_computation.50 | convolution fusion | flops 2415919104 | bytes 9437184 | tf_op jit(solution)/shard_map/dot_general | solution.py:53
  95.9 3.3 pad_maximum_fusion
  99.1 0.0 all-gather.15.cloned.1.call-start
  99.2 38.2 %reduce-scatter.9.cloned.1.call-done = f32[128,1536]{1,0:T(8,128)} async-done(((f32[512,1536]{1,0:T(8,128)}), f32[128,1536]{1,0:T(8,128)}) %reduce-scatter.9.cloned.1.call-update) | async-done | bytes 786448 | tf_op jit(solution)/shard_map/reduce_scatter | solution.py:83
  137.4 73.5 %reduce-scatter.5.cloned.1.call-done = f32[128,3072]{1,0:T(8,128)} async-done(((f32[512,3072]{1,0:T(8,128)}), f32[128,3072]{1,0:T(8,128)}) %reduce-scatter.5.cloned.1.call-update) | async-done | bytes 1572880 | tf_op jit(solution)/shard_map/reduce_scatter | solution.py:49
  210.9 3.0 multiply_convert_fusion
  213.9 0.0 all-gather.11.cloned.1.call-start
  214.0 0.7 all-gather.11.cloned.1.call-update
  214.7 0.0 all-gather.17.cloned.1.call-start
  214.7 0.7 all-gather.17.cloned.1.call-update
  215.4 0.0 reduce-scatter.11.cloned.1.call-start
  215.5 29.5 %all-gather.15.cloned.1.call-done = bf16[512,1536]{1,0:T(8,128)(2,1)} async-done(((bf16[128,1536]{1,0:T(8,128)(2,1)}), bf16[512,1536]{1,0:T(8,128)(2,1)}) %all-gather.15.cloned.1.call-update) | async-done | bytes 1572880 | tf_op jit(solution)/shard_map/all_gather | solution.py:88
  244.9 7.1 %fusion.28 = f32[512,1536]{1,0:T(8,128)} fusion(bf16[512,1536]{1,0:T(8,128)(2,1)} %all-gather.15.cloned.1.call-done, bf16[1536,1536]{1,0:T(8,128)(2,1)} %param.10), kind=kOutput, calls=%fused_computation.53 | convolution fusion | flops 2415919104 | bytes 9437184 | tf_op jit(solution)/shard_map/dot_general | solution.py:25
  252.1 0.2 reduce-scatter.7.cloned.1.call-start
  252.3 25.3 %all-gather.11.cloned.1.call-done = bf16[512,1536]{1,0:T(8,128)(2,1)} async-done(((bf16[128,1536]{1,0:T(8,128)(2,1)}), bf16[512,1536]{1,0:T(8,128)(2,1)}) %all-gather.11.cloned.1.call-update) | async-done | bytes 1572880 | tf_op jit(solution)/shard_map/all_gather | solution.py:75
  277.6 7.1 %fusion.26 = f32[512,1536]{1,0:T(8,128)} fusion(bf16[512,1536]{1,0:T(8,128)(2,1)} %all-gather.11.cloned.1.call-done, bf16[1536,1536]{1,0:T(8,128)(2,1)} %param.11), kind=kOutput, calls=%fused_computation.51 | convolution fusion | flops 2415919104 | bytes 9437184 | tf_op jit(solution)/shard_map/dot_general | solution.py:74
  284.8 1.4 copy-done.5
  286.2 0.5 copy-done.6
  286.7 6.0 %multiply_reduce_fusion.1 = (f32[]{:T(128)}, f32[1536,1536]{1,0:T(8,128)}) fusion(bf16[512,1536]{1,0:T(8,128)(2,1)S(1)} %copy-done.5, bf16[512,1536]{1,0:T(8,128)(2,1)S(1)} %copy-done.6), kind=kOutput, calls=%fused_computation.1 | convolution fusion | flops 2420637696 | bytes 12582916 | tf_op jit(solution)/shard_map/dot_general | solution.py:25
  292.7 18.2 %all-gather.17.cloned.1.call-done = bf16[512,1536]{1,0:T(8,128)(2,1)} async-done(((bf16[128,1536]{1,0:T(8,128)(2,1)}), bf16[512,1536]{1,0:T(8,128)(2,1)}) %all-gather.17.cloned.1.call-update) | async-done | bytes 1572880 | tf_op jit(solution)/shard_map/all_gather | solution.py:87
  310.9 8.9 %multiply_reduce_fusion = (f32[]{:T(128)}, f32[1536,1536]{1,0:T(8,128)}) fusion(bf16[512,1536]{1,0:T(8,128)(2,1)} %all-gather.17.cloned.1.call-done, bf16[512,1536]{1,0:T(8,128)(2,1)} %all-gather.13.cloned.1.call-done), kind=kOutput, calls=%fused_computation | convolution fusion | flops 2420637696 | bytes 12582916 | tf_op jit(solution)/shard_map/dot_general | solution.py:25
  321.1 32.5 %reduce-scatter.11.cloned.1.call-done = f32[64,1536]{1,0:T(8,128)} async-done(((f32[512,1536]{1,0:T(8,128)}), f32[64,1536]{1,0:T(8,128)}) %reduce-scatter.11.cloned.1.call-update) | async-done | bytes 393232 | tf_op jit(solution)/shard_map/reduce_scatter | solution.py:92
  353.6 1.4 fusion.17
  355.0 16.1 %psum.62 = f32[1536]{0:T(1024)S(1)} all-reduce(f32[1536]{0:T(1024)S(1)} %get-tuple-element.6), channel_id=1, replica_groups=mesh['row'=8,'col'=4] {'row'}, use_global_device_ids=true, to_apply=%region_19.0 | all-reduce | flops 1536 | bytes 12288 | tf_op jit(solution)/shard_map/psum | solution.py:104
  371.1 0.6 multiply_reduce_fusion.3
  372.3 38.8 %psum.63 = f32[]{:T(128)} all-reduce(f32[]{:T(128)S(6)} %add.60), channel_id=1, replica_groups=mesh['row'=8,'col'=4] {'row','col'}, use_global_device_ids=true, to_apply=%region_21.0 | all-reduce | flops 1 | bytes 8 | tf_op jit(solution)/shard_map/psum | solution.py:106
  411.9 9.9 %all-reduce = (f32[64]{0:T(128)S(1)}, f32[64]{0:T(128)S(1)}) all-reduce(f32[64]{0:T(128)S(1)} %get-tuple-element.7, f32[64]{0:T(128)S(1)} %get-tuple-element.8), channel_id=1, replica_groups=mesh['row'=8,'col'=4] {'col'}, use_global_device_ids=true, to_apply=%region_15.0 | all-reduce | flops 128 | bytes 1024 | tf_op jit(solution)/shard_map/psum | solution.py:96
  421.8 0.6 broadcast_multiply_fusion.2
  422.5 8.7 %broadcast_multiply_fusion = f32[1536,1536]{1,0:T(8,128)} fusion(f32[1536,1536]{1,0:T(8,128)} %get-tuple-element.31, f32[]{:T(128)S(6)} %min.3), kind=kLoop, calls=%fused_computation.3 | loop fusion | flops 2359296 | bytes 18874372 | tf_op jit(solution)/shard_map/mul | solution.py:111
  431.2 4.8 %broadcast_multiply_fusion.1 = f32[1536,1536]{1,0:T(8,128)} fusion(f32[1536,1536]{1,0:T(8,128)S(1)} %bitcast.15, f32[]{:T(128)S(6)} %min.3), kind=kLoop, calls=%fused_computation.4 | loop fusion | flops 2359296 | bytes 18874372 | tf_op jit(solution)/shard_map/mul | solution.py:111
  436.0 1.7 fusion.23
  437.7 0.9 fusion.16
  (29 shorter events, 0.2 us)
Async XLA Ops:
  7.2 30.5 %all-gather.13.cloned.1.call-start = ((), (), s32[]{:S(2)}) async-start(), calls=%async_computation.9 | async-start | bytes 1769472 | tf_op jit(solution)/shard_map/all_gather | solution.py:82
  7.9 56.4 %all-gather.7.cloned.1.call-start = ((), (), s32[]{:S(2)}) async-start(), calls=%async_computation.4 | async-start | bytes 1769472 | tf_op jit(solution)/shard_map/all_gather | solution.py:45
  23.6 67.3 %all-gather.9.cloned.1.call-start = ((), (), s32[]{:S(2)}) async-start(), calls=%async_computation.5 | async-start | bytes 1769472 | tf_op jit(solution)/shard_map/all_gather | solution.py:46
  24.3 113.1 %reduce-scatter.9.cloned.1.call-start = ((), (), s32[]{:S(2)}) async-start(), calls=%async_computation.10 | async-start | bytes 3932160 | tf_op jit(solution)/shard_map/reduce_scatter | solution.py:83
  44.8 166.1 %reduce-scatter.5.cloned.1.call-start = ((), (), s32[]{:S(2)}) async-start(), calls=%async_computation.6 | async-start | bytes 7864320 | tf_op jit(solution)/shard_map/reduce_scatter | solution.py:49
  99.1 145.8 %all-gather.15.cloned.1.call-start = ((), (), s32[]{:S(2)}) async-start(), calls=%async_computation.11 | async-start | bytes 1966080 | tf_op jit(solution)/shard_map/all_gather | solution.py:88
  213.9 63.7 %all-gather.11.cloned.1.call-start = ((), (), s32[]{:S(2)}) async-start(), calls=%async_computation.7 | async-start | bytes 1966080 | tf_op jit(solution)/shard_map/all_gather | solution.py:75
  214.7 96.2 %all-gather.17.cloned.1.call-start = ((), (), s32[]{:S(2)}) async-start(), calls=%async_computation.13 | async-start | bytes 1966080 | tf_op jit(solution)/shard_map/all_gather | solution.py:87
  215.4 138.2 %reduce-scatter.11.cloned.1.call-start = ((), (), s32[]{:S(2)}) async-start(), calls=%async_computation.12 | async-start | bytes 3538944 | tf_op jit(solution)/shard_map/reduce_scatter | solution.py:92
  252.1 183.9 %reduce-scatter.7.cloned.1.call-start = ((), (), s32[]{:S(2)}) async-start(), calls=%async_computation.8 | async-start | bytes 3538944 | tf_op jit(solution)/shard_map/reduce_scatter | solution.py:79
  284.8 1.4 copy-start.5
  284.8 1.9 copy-start.6
  292.7 60.9 %copy-start = (bf16[64,1536]{1,0:T(8,128)(2,1)S(1)}, bf16[64,1536]{1,0:T(8,128)(2,1)}, u32[]{:S(2)}) copy-start(bf16[64,1536]{1,0:T(8,128)(2,1)} %param.7) | copy-start | bytes 589828
  292.7 60.9 %copy-start.4 = (f32[1536]{0:T(1024)S(1)}, f32[1536]{0:T(1024)}, u32[]{:S(2)}) copy-start(f32[1536]{0:T(1024)} %param.9) | copy-start | bytes 18436
  353.6 77.5 %slice-start = ((s8[9437184]{0:T(1024)(128)(4,1)}), s8[1048576]{0:T(1024)(128)(4,1)S(1)}, s32[]{:S(2)}) async-start(s8[9437184]{0:T(1024)(128)(4,1)} %bitcast.14), calls=%async_computation.14 | async-start | bytes 2097152
  422.4 8.7 %slice-start.1 = ((s8[9437184]{0:T(1024)(128)(4,1)}), s8[4194304]{0:T(1024)(128)(4,1)S(1)}, s32[]{:S(2)}) async-start(s8[9437184]{0:T(1024)(128)(4,1)} %bitcast.14), calls=%async_computation.15 | async-start | bytes 8388608
  422.4 8.7 %slice-start.2 = ((s8[9437184]{0:T(1024)(128)(4,1)}), s8[4194304]{0:T(1024)(128)(4,1)S(1)}, s32[]{:S(2)}) async-start(s8[9437184]{0:T(1024)(128)(4,1)} %bitcast.14), calls=%async_computation.16 | async-start | bytes 8388608
  431.1 4.8 %copy-start.1 = (bf16[64,1536]{1,0:T(8,128)(2,1)S(1)}, bf16[64,1536]{1,0:T(8,128)(2,1)}, u32[]{:S(2)}) copy-start(bf16[64,1536]{1,0:T(8,128)(2,1)} %param.6) | copy-start | bytes 589828
  431.2 6.5 %copy-start.2 = (f32[64,1536]{1,0:T(8,128)S(1)}, f32[64,1536]{1,0:T(8,128)}, u32[]{:S(2)}) copy-start(f32[64,1536]{1,0:T(8,128)} %reduce-scatter.11.cloned.1.call-done) | copy-start | bytes 1179652
  431.2 6.5 %copy-start.3 = (bf16[64,1536]{1,0:T(8,128)(2,1)S(1)}, bf16[64,1536]{1,0:T(8,128)(2,1)}, u32[]{:S(2)}) copy-start(bf16[64,1536]{1,0:T(8,128)(2,1)} %param.8) | copy-start | bytes 589828
Sparse Core Ops, SparseCore 0:
  9.6 27.9 all-gather.12
  39.8 24.3 all-gather.6
  66.5 24.3 all-gather.8
  94.3 43.0 reduce-scatter.8
  140.8 70.0 reduce-scatter.4
  214.0 30.8 all-gather.14
  246.8 30.8 all-gather.10
  280.0 30.8 all-gather.16
  313.2 40.3 reduce-scatter.10
  355.8 40.2 reduce-scatter.6
where the time goes:
time: 447 us
  waiting for transfers between devices  274 us (61%)
  blocking collectives  76.2 us (17%)
  matrix products  46.1 us (10%)
  other arithmetic  29.2 us (7%)
  between operations  18.1 us (4%)
    reduce_scatter x1, waiting for transfers between devices, up_both(): lax.psum_scatter(jnp.concatenate([jnp.dot(full_a, w_up, preferred_element...  73.5 us
    psum x1, blocking collectives, on_device(): lax.psum(weight_squares + first_row * jnp.sum(g_gain * g_gain), ('row', '...  38.8 us
    reduce_scatter x1, waiting for transfers between devices, on_device(): lax.psum_scatter(contract(grad_full, w_down, 1, 1), 'col', scatter_dimens...  38.2 us
    reduce_scatter x1, waiting for transfers between devices, on_device(): lax.psum_scatter(input_total, 'row', scatter_dimension=0, tiled=True)  32.5 us
    all_gather x1, waiting for transfers between devices, on_device(): pre_piece = lax.all_gather(grad_pre, 'col', axis=0, tiled=True)  29.5 us
    dot_general x4, matrix products, contract(): lax.dot_general(left, right, (((left_dim,), (right_dim,)), ((), ())), pre...  29.2 us
    all_gather x1, waiting for transfers between devices, on_device(): lax.all_gather(hidden_a, 'col', axis=0, tiled=True)  25.3 us
    all_gather x1, waiting for transfers between devices, up_both(): lax.all_gather(normed_b, 'row', axis=0, tiled=True)  21.7 us
  transfers between devices with their start and end apart: 10, of which 9 were waited for; matrix products, arithmetic and copies ran while one was open for 16% of the time, Pallas kernels for 0%

commit v1 on v0

--- a/solution.py
+++ b/solution.py
@@ -103,7 +103,7 @@
     weight_squares = jnp.sum(up_total * up_total) + jnp.sum(down_total * down_total)
     g_gain = lax.psum(gain_part, "row")
     first_row = (lax.axis_index("row") == 0).astype(jnp.float32)
-    total = lax.psum(weight_squares + first_row * jnp.sum(g_gain * g_gain), ("row", "col"))
+    total = lax.psum(lax.psum(weight_squares + first_row * jnp.sum(g_gain * g_gain), "col"), "row")
     param_count = 2 * D * FF + D
     norm_value = jnp.sqrt(total)
     grad_rms = norm_value / math.sqrt(param_count)

time: 447 us -> 423 us (0.946)
  blocking collectives: 76.2 us -> 52.5 us
    psum x1, blocking collectives: 38.8 us -> 14.5 us  [on_device(): lax.psum(lax.psum(weight_squares + first_row * jnp.sum(g_gain * g_gain),...]
where the time goes in v1:
time: 423 us
  waiting for transfers between devices  275 us (65%)
  blocking collectives  52.5 us (12%)
  matrix products  45.9 us (11%)
  other arithmetic  29.2 us (7%)
  between operations  18.1 us (4%)
    reduce_scatter x1, waiting for transfers between devices, up_both(): lax.psum_scatter(jnp.concatenate([jnp.dot(full_a, w_up, preferred_element...  73.5 us
    reduce_scatter x1, waiting for transfers between devices, on_device(): lax.psum_scatter(contract(grad_full, w_down, 1, 1), 'col', scatter_dimens...  38.2 us
    reduce_scatter x1, waiting for transfers between devices, on_device(): lax.psum_scatter(input_total, 'row', scatter_dimension=0, tiled=True)  33.2 us
    all_gather x1, waiting for transfers between devices, on_device(): pre_piece = lax.all_gather(grad_pre, 'col', axis=0, tiled=True)  29.5 us
    dot_general x4, matrix products, contract(): lax.dot_general(left, right, (((left_dim,), (right_dim,)), ((), ())), pre...  29 us
    all_gather x1, waiting for transfers between devices, on_device(): lax.all_gather(hidden_a, 'col', axis=0, tiled=True)  25.3 us
    all_gather x1, waiting for transfers between devices, up_both(): lax.all_gather(normed_a, 'row', axis=0, tiled=True)  21.7 us
    all_gather x1, waiting for transfers between devices, up_both(): lax.all_gather(normed_b, 'row', axis=0, tiled=True)  19.5 us
  transfers between devices with their start and end apart: 10, of which 9 were waited for; matrix products, arithmetic and copies ran while one was open for 16% of the time, Pallas kernels for 0%

profile of v1, /device:TPU:0, one launch (start us, length us, event | category | flops | bytes accessed | tf_op | source)
XLA Modules:
  0.0 422.9 jit_solution(17916136469980131166)
XLA Ops:
  7.2 0.0 all-gather.13.cloned.1.call-start
  7.2 0.7 all-gather.13.cloned.1.call-update
  7.9 0.0 all-gather.9.cloned.1.call-start
  7.9 1.1 convert_reduce_fusion.1
  9.0 1.1 convert_reduce_fusion
  10.1 11.4 %all-reduce.1 = (f32[64]{0:T(128)S(1)}, f32[64]{0:T(128)S(1)}, f32[64]{0:T(128)S(1)}, f32[64]{0:T(128)S(1)}) all-reduce(f32[64]{0:T(128)S(1)} %get-tuple-element.12, f32[64]{0:T(128)S(1)} %get-tuple-element.11, f32[64]{0:T(128)S(1)} %get-tuple-element.10, f32[64]{0:T(128)S(1)} %get-tuple-element.9), channel_id=1, replica_groups=mesh['row'=8,'col'=4] {'col'}, use_global_device_ids=true, to_apply=%region_7.0 | all-reduce | flops 256 | bytes 2048 | tf_op jit(solution)/shard_map/psum | solution.py:67
  21.5 2.0 fusion.21
  23.6 0.0 all-gather.7.cloned.1.call-start
  23.6 0.7 all-gather.7.cloned.1.call-update
  24.3 0.0 reduce-scatter.9.cloned.1.call-start
  24.4 13.3 %all-gather.13.cloned.1.call-done = bf16[512,1536]{1,0:T(8,128)(2,1)} async-done(((bf16[64,1536]{1,0:T(8,128)(2,1)}), bf16[512,1536]{1,0:T(8,128)(2,1)}) %all-gather.13.cloned.1.call-update) | async-done | bytes 1572880 | tf_op jit(solution)/shard_map/all_gather | solution.py:82
  37.6 7.1 %fusion.27 = f32[512,1536]{1,0:T(8,128)} fusion(bf16[512,1536]{1,0:T(8,128)(2,1)} %all-gather.13.cloned.1.call-done, bf16[1536,1536]{1,0:T(8,128)(2,1)} %param.11), kind=kOutput, calls=%fused_computation.52 | convolution fusion | flops 2415919104 | bytes 9437184 | tf_op jit(solution)/shard_map/dot_general | solution.py:25
  44.8 0.0 reduce-scatter.5.cloned.1.call-start
  44.8 19.5 %all-gather.9.cloned.1.call-done = bf16[512,1536]{1,0:T(8,128)(2,1)} async-done(((bf16[64,1536]{1,0:T(8,128)(2,1)}), bf16[512,1536]{1,0:T(8,128)(2,1)}) %all-gather.9.cloned.1.call-update) | async-done | bytes 1572880 | tf_op jit(solution)/shard_map/all_gather | solution.py:46
  64.3 4.9 %fusion.25 = f32[512,1536]{1,0:T(8,128)S(1)} fusion(bf16[512,1536]{1,0:T(8,128)(2,1)} %all-gather.9.cloned.1.call-done, bf16[1536,1536]{1,0:T(8,128)(2,1)} %param.10), kind=kOutput, calls=%fused_computation.50 | convolution fusion | flops 2415919104 | bytes 9437184 | tf_op jit(solution)/shard_map/dot_general | solution.py:53
  69.2 21.7 %all-gather.7.cloned.1.call-done = bf16[512,1536]{1,0:T(8,128)(2,1)} async-done(((bf16[64,1536]{1,0:T(8,128)(2,1)}), bf16[512,1536]{1,0:T(8,128)(2,1)}) %all-gather.7.cloned.1.call-update) | async-done | bytes 1572880 | tf_op jit(solution)/shard_map/all_gather | solution.py:45
  90.9 4.9 %fusion.24 = f32[512,1536]{1,0:T(8,128)S(1)} fusion(bf16[512,1536]{1,0:T(8,128)(2,1)} %all-gather.7.cloned.1.call-done, bf16[1536,1536]{1,0:T(8,128)(2,1)} %param.10), kind=kOutput, calls=%fused_computation.49 | convolution fusion | flops 2415919104 | bytes 9437184 | tf_op jit(solution)/shard_map/dot_general | solution.py:52
  95.8 3.3 pad_maximum_fusion
  99.1 0.0 all-gather.15.cloned.1.call-start
  99.2 38.2 %reduce-scatter.9.cloned.1.call-done = f32[128,1536]{1,0:T(8,128)} async-done(((f32[512,1536]{1,0:T(8,128)}), f32[128,1536]{1,0:T(8,128)}) %reduce-scatter.9.cloned.1.call-update) | async-done | bytes 786448 | tf_op jit(solution)/shard_map/reduce_scatter | solution.py:83
  137.4 73.5 %reduce-scatter.5.cloned.1.call-done = f32[128,3072]{1,0:T(8,128)} async-done(((f32[512,3072]{1,0:T(8,128)}), f32[128,3072]{1,0:T(8,128)}) %reduce-scatter.5.cloned.1.call-update) | async-done | bytes 1572880 | tf_op jit(solution)/shard_map/reduce_scatter | solution.py:49
  210.9 3.0 multiply_convert_fusion
  213.9 0.0 all-gather.11.cloned.1.call-start
  214.0 0.7 all-gather.11.cloned.1.call-update
  214.7 0.0 all-gather.17.cloned.1.call-start
  214.7 0.7 all-gather.17.cloned.1.call-update
  215.4 0.0 reduce-scatter.11.cloned.1.call-start
  215.5 29.5 %all-gather.15.cloned.1.call-done = bf16[512,1536]{1,0:T(8,128)(2,1)} async-done(((bf16[128,1536]{1,0:T(8,128)(2,1)}), bf16[512,1536]{1,0:T(8,128)(2,1)}) %all-gather.15.cloned.1.call-update) | async-done | bytes 1572880 | tf_op jit(solution)/shard_map/all_gather | solution.py:88
  244.9 7.1 %fusion.28 = f32[512,1536]{1,0:T(8,128)} fusion(bf16[512,1536]{1,0:T(8,128)(2,1)} %all-gather.15.cloned.1.call-done, bf16[1536,1536]{1,0:T(8,128)(2,1)} %param.10), kind=kOutput, calls=%fused_computation.53 | convolution fusion | flops 2415919104 | bytes 9437184 | tf_op jit(solution)/shard_map/dot_general | solution.py:25
  252.1 0.2 reduce-scatter.7.cloned.1.call-start
  252.3 25.3 %all-gather.11.cloned.1.call-done = bf16[512,1536]{1,0:T(8,128)(2,1)} async-done(((bf16[128,1536]{1,0:T(8,128)(2,1)}), bf16[512,1536]{1,0:T(8,128)(2,1)}) %all-gather.11.cloned.1.call-update) | async-done | bytes 1572880 | tf_op jit(solution)/shard_map/all_gather | solution.py:75
  277.7 7.0 %fusion.26 = f32[512,1536]{1,0:T(8,128)} fusion(bf16[512,1536]{1,0:T(8,128)(2,1)} %all-gather.11.cloned.1.call-done, bf16[1536,1536]{1,0:T(8,128)(2,1)} %param.11), kind=kOutput, calls=%fused_computation.51 | convolution fusion | flops 2415919104 | bytes 9437184 | tf_op jit(solution)/shard_map/dot_general | solution.py:74
  284.7 1.4 copy-done.5
  286.2 0.6 copy-done.6
  286.7 6.0 %multiply_reduce_fusion.1 = (f32[]{:T(128)}, f32[1536,1536]{1,0:T(8,128)}) fusion(bf16[512,1536]{1,0:T(8,128)(2,1)S(1)} %copy-done.5, bf16[512,1536]{1,0:T(8,128)(2,1)S(1)} %copy-done.6), kind=kOutput, calls=%fused_computation.1 | convolution fusion | flops 2420637696 | bytes 12582916 | tf_op jit(solution)/shard_map/dot_general | solution.py:25
  292.8 17.6 %all-gather.17.cloned.1.call-done = bf16[512,1536]{1,0:T(8,128)(2,1)} async-done(((bf16[128,1536]{1,0:T(8,128)(2,1)}), bf16[512,1536]{1,0:T(8,128)(2,1)}) %all-gather.17.cloned.1.call-update) | async-done | bytes 1572880 | tf_op jit(solution)/shard_map/all_gather | solution.py:87
  310.4 8.8 %multiply_reduce_fusion = (f32[]{:T(128)}, f32[1536,1536]{1,0:T(8,128)}) fusion(bf16[512,1536]{1,0:T(8,128)(2,1)} %all-gather.17.cloned.1.call-done, bf16[512,1536]{1,0:T(8,128)(2,1)} %all-gather.13.cloned.1.call-done), kind=kOutput, calls=%fused_computation | convolution fusion | flops 2420637696 | bytes 12582916 | tf_op jit(solution)/shard_map/dot_general | solution.py:25
  320.4 33.2 %reduce-scatter.11.cloned.1.call-done = f32[64,1536]{1,0:T(8,128)} async-done(((f32[512,1536]{1,0:T(8,128)}), f32[64,1536]{1,0:T(8,128)}) %reduce-scatter.11.cloned.1.call-update) | async-done | bytes 393232 | tf_op jit(solution)/shard_map/reduce_scatter | solution.py:92
  353.7 1.4 fusion.17
  355.0 16.1 %psum.69 = f32[1536]{0:T(1024)S(1)} all-reduce(f32[1536]{0:T(1024)S(1)} %get-tuple-element.6), channel_id=1, replica_groups=mesh['row'=8,'col'=4] {'row'}, use_global_device_ids=true, to_apply=%region_19.0 | all-reduce | flops 1536 | bytes 12288 | tf_op jit(solution)/shard_map/psum | solution.py:104
  371.1 0.6 multiply_reduce_fusion.3
  372.3 10.6 %all-reduce = (f32[64]{0:T(128)S(1)}, f32[64]{0:T(128)S(1)}, f32[]{:T(128)}) all-reduce(f32[64]{0:T(128)S(1)} %get-tuple-element.7, f32[64]{0:T(128)S(1)} %get-tuple-element.8, f32[]{:T(128)S(6)} %add.62), channel_id=1, replica_groups=mesh['row'=8,'col'=4] {'col'}, use_global_device_ids=true, to_apply=%region_15.0 | all-reduce | flops 129 | bytes 1032 | tf_op jit(solution)/shard_map/psum | solution.py:96
  382.9 14.5 %psum.71 = f32[]{:T(128)} all-reduce(f32[]{:T(128)} %get-tuple-element.15), channel_id=1, replica_groups=mesh['row'=8,'col'=4] {'row'}, use_global_device_ids=true, to_apply=%region_22.0 | all-reduce | flops 1 | bytes 8 | tf_op jit(solution)/shard_map/psum | solution.py:106
  398.1 0.6 broadcast_multiply_fusion.2
  398.8 8.7 %broadcast_multiply_fusion.1 = f32[1536,1536]{1,0:T(8,128)} fusion(f32[1536,1536]{1,0:T(8,128)} %get-tuple-element.30, f32[]{:T(128)S(6)} %min.3), kind=kLoop, calls=%fused_computation.4 | loop fusion | flops 2359296 | bytes 18874372 | tf_op jit(solution)/shard_map/mul | solution.py:111
  407.5 4.8 %broadcast_multiply_fusion = f32[1536,1536]{1,0:T(8,128)} fusion(f32[1536,1536]{1,0:T(8,128)S(1)} %bitcast.15, f32[]{:T(128)S(6)} %min.3), kind=kLoop, calls=%fused_computation.3 | loop fusion | flops 2359296 | bytes 18874372 | tf_op jit(solution)/shard_map/mul | solution.py:111
  412.3 1.7 fusion.23
  414.0 0.9 fusion.16
  (29 shorter events, 0.2 us)
Async XLA Ops:
  7.2 30.5 %all-gather.13.cloned.1.call-start = ((), (), s32[]{:S(2)}) async-start(), calls=%async_computation.9 | async-start | bytes 1769472 | tf_op jit(solution)/shard_map/all_gather | solution.py:82
  7.9 56.4 %all-gather.9.cloned.1.call-start = ((), (), s32[]{:S(2)}) async-start(), calls=%async_computation.5 | async-start | bytes 1769472 | tf_op jit(solution)/shard_map/all_gather | solution.py:46
  23.6 67.3 %all-gather.7.cloned.1.call-start = ((), (), s32[]{:S(2)}) async-start(), calls=%async_computation.4 | async-start | bytes 1769472 | tf_op jit(solution)/shard_map/all_gather | solution.py:45
  24.3 113.1 %reduce-scatter.9.cloned.1.call-start = ((), (), s32[]{:S(2)}) async-start(), calls=%async_computation.10 | async-start | bytes 3932160 | tf_op jit(solution)/shard_map/reduce_scatter | solution.py:83
  44.8 166.1 %reduce-scatter.5.cloned.1.call-start = ((), (), s32[]{:S(2)}) async-start(), calls=%async_computation.6 | async-start | bytes 7864320 | tf_op jit(solution)/shard_map/reduce_scatter | solution.py:49
  99.1 145.8 %all-gather.15.cloned.1.call-start = ((), (), s32[]{:S(2)}) async-start(), calls=%async_computation.11 | async-start | bytes 1966080 | tf_op jit(solution)/shard_map/all_gather | solution.py:88
  213.9 63.7 %all-gather.11.cloned.1.call-start = ((), (), s32[]{:S(2)}) async-start(), calls=%async_computation.7 | async-start | bytes 1966080 | tf_op jit(solution)/shard_map/all_gather | solution.py:75
  214.7 95.7 %all-gather.17.cloned.1.call-start = ((), (), s32[]{:S(2)}) async-start(), calls=%async_computation.13 | async-start | bytes 1966080 | tf_op jit(solution)/shard_map/all_gather | solution.py:87
  215.4 138.2 %reduce-scatter.11.cloned.1.call-start = ((), (), s32[]{:S(2)}) async-start(), calls=%async_computation.12 | async-start | bytes 3538944 | tf_op jit(solution)/shard_map/reduce_scatter | solution.py:92
  252.1 160.2 %reduce-scatter.7.cloned.1.call-start = ((), (), s32[]{:S(2)}) async-start(), calls=%async_computation.8 | async-start | bytes 3538944 | tf_op jit(solution)/shard_map/reduce_scatter | solution.py:79
  284.7 1.4 copy-start.5
  284.7 2.0 copy-start.6
  292.8 60.9 %copy-start = (bf16[64,1536]{1,0:T(8,128)(2,1)S(1)}, bf16[64,1536]{1,0:T(8,128)(2,1)}, u32[]{:S(2)}) copy-start(bf16[64,1536]{1,0:T(8,128)(2,1)} %param.7) | copy-start | bytes 589828
  292.8 60.9 %copy-start.4 = (f32[1536]{0:T(1024)S(1)}, f32[1536]{0:T(1024)}, u32[]{:S(2)}) copy-start(f32[1536]{0:T(1024)} %param.9) | copy-start | bytes 18436
  353.7 53.8 %slice-start = ((s8[9437184]{0:T(1024)(128)(4,1)}), s8[1048576]{0:T(1024)(128)(4,1)S(1)}, s32[]{:S(2)}) async-start(s8[9437184]{0:T(1024)(128)(4,1)} %bitcast.14), calls=%async_computation.14 | async-start | bytes 2097152
  398.7 8.7 %slice-start.1 = ((s8[9437184]{0:T(1024)(128)(4,1)}), s8[4194304]{0:T(1024)(128)(4,1)S(1)}, s32[]{:S(2)}) async-start(s8[9437184]{0:T(1024)(128)(4,1)} %bitcast.14), calls=%async_computation.15 | async-start | bytes 8388608
  398.8 8.7 %slice-start.2 = ((s8[9437184]{0:T(1024)(128)(4,1)}), s8[4194304]{0:T(1024)(128)(4,1)S(1)}, s32[]{:S(2)}) async-start(s8[9437184]{0:T(1024)(128)(4,1)} %bitcast.14), calls=%async_computation.16 | async-start | bytes 8388608
  407.4 4.8 %copy-start.1 = (bf16[64,1536]{1,0:T(8,128)(2,1)S(1)}, bf16[64,1536]{1,0:T(8,128)(2,1)}, u32[]{:S(2)}) copy-start(bf16[64,1536]{1,0:T(8,128)(2,1)} %param.6) | copy-start | bytes 589828
  407.5 6.5 %copy-start.2 = (f32[64,1536]{1,0:T(8,128)S(1)}, f32[64,1536]{1,0:T(8,128)}, u32[]{:S(2)}) copy-start(f32[64,1536]{1,0:T(8,128)} %reduce-scatter.11.cloned.1.call-done) | copy-start | bytes 1179652
  407.5 6.5 %copy-start.3 = (bf16[64,1536]{1,0:T(8,128)(2,1)S(1)}, bf16[64,1536]{1,0:T(8,128)(2,1)}, u32[]{:S(2)}) copy-start(bf16[64,1536]{1,0:T(8,128)(2,1)} %param.8) | copy-start | bytes 589828
Sparse Core Ops, SparseCore 0:
  9.6 27.9 all-gather.12
  39.8 24.3 all-gather.8
  66.5 24.3 all-gather.6
  94.3 43.0 reduce-scatter.8
  140.8 70.0 reduce-scatter.4
  214.1 30.8 all-gather.14
  246.8 30.8 all-gather.10
  279.5 30.8 all-gather.16
  313.2 40.3 reduce-scatter.10
  355.8 40.1 reduce-scatter.6
